TPU v7x, 128 devices: a whole 4x4x4 slice. The times are simulated.
128 devices in a mesh: grp: 4 (over z), seq: 32 (over x, y, core).
Axes of the slice: x: 4, y: 4, z: 4, core: 2. Of those that a mesh axis runs over, the one named last changes fastest.
Arguments:
- hidden_in: bfloat16 [96, 4096], P(None, ('grp', 'seq')), may hold values from -6 to 6
- norm_gain: float32 [4096], replicated, may hold values from 0.5 to 1.5
- w_ssm_in: bfloat16 [4096, 8192], P(None, ('grp', 'seq')), may hold values from -0.09375 to 0.09375
- w_ssm_gate: bfloat16 [4096, 8192], P(None, ('grp', 'seq')), may hold values from -0.09375 to 0.09375
- conv_weight: float32 [4, 8192], P(None, ('grp', 'seq')), may hold values from -3 to 3
- conv_bias: float32 [8192], P(('grp', 'seq')), may hold values from -0.5 to 0.5
- conv_state: bfloat16 [96, 3, 8192], P(None, None, ('grp', 'seq')), may hold values from -6 to 6
- w_state_proj: bfloat16 [8192, 288], P(('grp', 'seq')), may hold values from -0.0625 to 0.0625
- w_step: bfloat16 [256, 8192], P(None, ('grp', 'seq')), may hold values from -0.375 to 0.375
- step_bias: float32 [8192], P(('grp', 'seq')), may hold values from -4 to -1
- log_decay: float32 [16, 8192], P(None, ('grp', 'seq')), may hold values from 0 to 2.7
- skip_gain: float32 [8192], P(('grp', 'seq')), may hold values from 0.5 to 1.5
- ssm_state: float32 [96, 16, 8192], P(None, None, ('grp', 'seq')), may hold values from -6 to 6
- w_ssm_out: bfloat16 [8192, 4096], P(('grp', 'seq')), may hold values from -0.25 to 0.25
- w_query: bfloat16 [4096, 2048], P(None, 'grp'), may hold values from -6 to 6
- key_projection: bfloat16 [4096, 1024], P(None, 'grp'), may hold values from -0.09375 to 0.09375
- value_projection: bfloat16 [4096, 1024], P(None, 'grp'), may hold values from -0.09375 to 0.09375
- w_attn_out: bfloat16 [2048, 4096], P('grp', 'seq'), may hold values from -0.125 to 0.125
- w_mlp_gate: bfloat16 [4096, 14336], P(None, ('grp', 'seq')), may hold values from -0.09375 to 0.09375
- w_mlp_up: bfloat16 [4096, 14336], P(None, ('grp', 'seq')), may hold values from -0.09375 to 0.09375
- w_mlp_down: bfloat16 [14336, 4096], P(('grp', 'seq')), may hold values from -0.1875 to 0.1875
- cached_inputs: bfloat16 [96, 512, 4096], P('seq'), may hold values from -6 to 6
- window_lengths: int32 [96], replicated, may hold values from 1 to 512, as said below
Outputs:
- hidden_out: bfloat16 [96, 4096], P(None, ('grp', 'seq'))
- state_out: float32 [96, 16, 8192], P(None, None, ('grp', 'seq'))
Inputs may be any that keep to these rules, and one draw needn't show every extreme that they name: `window_lengths`: every sequence has at least one valid cached position, and some sequence fills the whole window of 512.
All inputs are finite; a program needn't handle non-finite values.
Results may differ from a plain program's by a relative error of at most 0.012.
The roundings to bfloat16 on the way count: a program that leaves them out, or rounds other values in their place, can miss the bound.
Values may be sent and summed in bfloat16 or wider, within the bound.
A program may use at most 128 MiB of HBM per device.

v0:
```python
import jax
import jax.numpy as jnp
from jax import lax
from jax.sharding import Mesh
from jax.sharding import PartitionSpec as P

HEAD_SIZE = 128
GRP_SEQ = ("grp", "seq_0", "seq_1", "seq_2")
SEQ = ("seq_0", "seq_1", "seq_2")


epsilon = 1e-05
rope_base = 10000.0


def from_everyone(shard, axis):
    length = lax.axis_size(axis)
    return lax.all_to_all(
        jnp.broadcast_to(shard[None], (length, *shard.shape)), axis, 0, 0, tiled=True
    )


def in_order(parts, dim):
    lengths = list(parts.shape[1:])
    lengths[dim] *= parts.shape[0]
    return jnp.moveaxis(parts, 0, dim).reshape(lengths)


def gather_axes(shard, axes, dim):
    far, near = axes
    parts = from_everyone(from_everyone(shard, far), near)
    return in_order(parts.swapaxes(0, 1).reshape(-1, *shard.shape), dim)


def cut_along(shard, dim, length):
    before, after = (shard.shape[:dim], shard.shape[dim + 1 :])
    return jnp.moveaxis(shard.reshape(*before, length, -1, *after), dim, 0)


def summed_on_arrival(shard, axis, dim):
    length = lax.axis_size(axis)
    parts = lax.all_to_all(cut_along(shard, dim, length), axis, 0, 0, tiled=True)
    return jnp.sum(parts, axis=0)


def sum_by_axis(shard, axes, dim):
    far, near = axes
    own = summed_on_arrival(cut_along(shard, dim, lax.axis_size(far)), near, dim + 1)
    return jnp.sum(lax.all_to_all(own, far, 0, 0, tiled=True), axis=0)


def filled_up(lines, length):
    spare = -lines.shape[0] % length
    if not spare:
        return lines
    return jnp.concatenate([lines, jnp.zeros((spare, *lines.shape[1:]), lines.dtype)])


def sum_by_parts(shard, axes):
    lines = shard.reshape(-1)
    own = sum_by_axis(filled_up(lines, lax.axis_size(axes[0]) * lax.axis_size(axes[1])), axes, 0)
    whole = gather_axes(own, axes, 0)
    return whole[: len(lines)].reshape(shard.shape)


def collect(shard, axis, dim):
    return in_order(from_everyone(shard, axis), dim)


def sent_and_summed(shard, axis, dim):
    parts = cut_along(shard, dim, lax.axis_size(axis))
    arrived = lax.all_to_all(parts, axis, split_axis=0, concat_axis=0, tiled=True)
    return arrived.astype(jnp.float32).sum(axis=0)


def sum_in_two_steps(shard, axes, dim):
    far, near = axes
    parts = cut_along(shard, dim, lax.axis_size(far))
    nearer = sent_and_summed(parts, near, dim + 1)
    arrived = lax.all_to_all(
        nearer.astype(jnp.bfloat16), far, split_axis=0, concat_axis=0, tiled=True
    )
    return arrived.astype(jnp.float32).sum(axis=0)


def apply_rotary(head_values, positions):
    half_dim = head_values.shape[-1] // 2
    frequency = rope_base ** (
        -(jnp.arange(half_dim, dtype=jnp.float32) * 2.0) / head_values.shape[-1]
    )
    angles = positions[..., None, None] * frequency
    cosine = jnp.cos(angles)
    sine_part = jnp.sin(angles)
    front_half = head_values[..., :half_dim]
    back_half = head_values[..., half_dim:]
    return jnp.concatenate(
        [front_half * cosine - back_half * sine_part, back_half * cosine + front_half * sine_part],
        axis=-1,
    )


def per_device(
    hidden_in,
    norm_gain,
    w_ssm_in,
    w_ssm_gate,
    conv_weight,
    conv_bias,
    conv_state,
    w_state_proj,
    w_step,
    step_bias,
    log_decay,
    skip_gain,
    ssm_state,
    w_ssm_out,
    w_query,
    key_projection,
    value_projection,
    w_attn_out,
    w_mlp_gate,
    w_mlp_up,
    w_mlp_down,
    cached_inputs,
    window_lengths,
):
    batch_rows = hidden_in.shape[0]
    model_width = norm_gain.shape[0]
    hidden_f = hidden_in.astype(jnp.float32)
    raw_full = gather_axes(hidden_in, (("grp", "seq_0", "seq_1"), "seq_2"), 1).astype(jnp.float32)
    row_scale = lax.rsqrt(jnp.mean(raw_full * raw_full, axis=1, keepdims=True) + epsilon)
    normed_input = (raw_full * row_scale * norm_gain).astype(jnp.bfloat16)
    ssm_input = jnp.dot(normed_input, w_ssm_in, preferred_element_type=jnp.float32).astype(
        jnp.bfloat16
    )
    gate_input = jnp.dot(normed_input, w_ssm_gate, preferred_element_type=jnp.float32)
    past_inputs = conv_state.astype(jnp.float32)
    conv_sum = (
        conv_bias
        + jnp.sum(past_inputs * conv_weight[:-1][None], axis=1)
        + conv_weight[-1] * lax.optimization_barrier(ssm_input).astype(jnp.float32)
    )
    conv_out = jax.nn.silu(conv_sum)
    rank_size = w_step.shape[0]
    state_size = log_decay.shape[0]
    low_rank = sum_by_parts(
        jnp.dot(conv_out.astype(jnp.bfloat16), w_state_proj, preferred_element_type=jnp.float32),
        (("grp", "seq_0", "seq_1"), "seq_2"),
    )
    step_low = low_rank[:, :rank_size].astype(jnp.bfloat16)
    input_map = low_rank[:, rank_size : rank_size + state_size]
    output_map = low_rank[:, rank_size + state_size :]
    step_size = jax.nn.softplus(
        jnp.dot(step_low, w_step, preferred_element_type=jnp.float32) + step_bias
    )
    decay_rate = jnp.exp(log_decay)
    state_out = (
        jnp.exp(-step_size[:, None, :] * decay_rate[None]) * ssm_state
        + step_size[:, None, :] * input_map[:, :, None] * conv_out[:, None, :]
    )
    ssm_mixed = jnp.sum(state_out * output_map[:, :, None], axis=1) + skip_gain * conv_out
    ssm_gated = (ssm_mixed * jax.nn.silu(gate_input)).astype(jnp.bfloat16)
    ssm_term = jnp.dot(ssm_gated, w_ssm_out, preferred_element_type=jnp.float32)
    gate_act = jnp.dot(normed_input, w_mlp_gate, preferred_element_type=jnp.float32)
    up_act = jnp.dot(normed_input, w_mlp_up, preferred_element_type=jnp.float32)
    mlp_hidden = (jax.nn.silu(gate_act) * up_act).astype(jnp.bfloat16)
    mlp_term = jnp.dot(mlp_hidden, w_mlp_down, preferred_element_type=jnp.float32)
    own_seqs = cached_inputs.shape[0]
    window_size = cached_inputs.shape[1]
    seq_start = lax.axis_index(SEQ) * own_seqs
    normed_own = lax.dynamic_slice_in_dim(normed_input, seq_start, own_seqs, 0)
    lengths_own = lax.dynamic_slice_in_dim(window_lengths, seq_start, own_seqs, 0)
    heads_here = w_query.shape[1] // HEAD_SIZE
    kv_here = key_projection.shape[1] // HEAD_SIZE
    heads_per_group = heads_here // kv_here
    attention_scale = HEAD_SIZE ** (-0.5)
    fresh_position = lengths_own.astype(jnp.float32)
    query = apply_rotary(
        jnp.dot(normed_own, w_query, preferred_element_type=jnp.float32).reshape(
            own_seqs, heads_here, HEAD_SIZE
        ),
        fresh_position,
    ).astype(jnp.bfloat16)
    fresh_key = apply_rotary(
        jnp.dot(normed_own, key_projection, preferred_element_type=jnp.float32).reshape(
            own_seqs, kv_here, HEAD_SIZE
        ),
        fresh_position,
    ).astype(jnp.bfloat16)
    fresh_value = (
        jnp.dot(normed_own, value_projection, preferred_element_type=jnp.float32)
        .astype(jnp.bfloat16)
        .reshape(own_seqs, kv_here, HEAD_SIZE)
    )
    flat_inputs = cached_inputs.reshape(own_seqs * window_size, model_width)
    slot_ids = jnp.arange(window_size, dtype=jnp.int32)
    positions = jnp.broadcast_to(slot_ids[None, :], (own_seqs, window_size)).astype(jnp.float32)
    window_key_rows = jnp.dot(
        flat_inputs, key_projection, preferred_element_type=jnp.float32
    ).reshape(own_seqs, window_size, kv_here, HEAD_SIZE)
    window_key_rows = apply_rotary(window_key_rows, positions).astype(jnp.bfloat16)
    window_value_rows = (
        jnp.dot(flat_inputs, value_projection, preferred_element_type=jnp.float32)
        .astype(jnp.bfloat16)
        .reshape(own_seqs, window_size, kv_here, HEAD_SIZE)
    )
    grouped_query = query.astype(jnp.float32).reshape(own_seqs, kv_here, heads_per_group, HEAD_SIZE)
    scores = (
        jnp.einsum("bkgd,bpkd->bkgp", grouped_query, window_key_rows.astype(jnp.float32))
        * attention_scale
    )
    fresh_score = (
        jnp.einsum("ynow,ynw->yno", grouped_query, fresh_key.astype(jnp.float32)) * attention_scale
    )
    is_valid = (slot_ids[None, :] < lengths_own[:, None])[:, None, None, :]
    scores = jnp.where(is_valid, scores, -1e30)
    joint_max = jnp.maximum(jnp.max(scores, axis=-1), fresh_score)
    weights = jnp.where(is_valid, jnp.exp(scores - joint_max[..., None]), 0.0)
    weight_new = jnp.exp(fresh_score - joint_max)
    joint_total = jnp.sum(weights, axis=-1) + weight_new
    joint_sum = (
        jnp.einsum("bkgp,bpkd->bkgd", weights, window_value_rows.astype(jnp.float32))
        + weight_new[..., None] * fresh_value.astype(jnp.float32)[:, :, None, :]
    )
    attended_own = (
        (joint_sum / joint_total[..., None])
        .reshape(own_seqs, heads_here * HEAD_SIZE)
        .astype(jnp.bfloat16)
    )
    attended = collect(attended_own, SEQ, 0)
    attn_cols = jnp.dot(attended, w_attn_out, preferred_element_type=jnp.float32)
    col_start = lax.axis_index(SEQ) * w_attn_out.shape[1]
    attn_term = lax.dynamic_update_slice(
        jnp.zeros((batch_rows, model_width), jnp.float32), attn_cols, (jnp.int32(0), col_start)
    )
    other_terms = mlp_term + attn_term
    summed = sum_in_two_steps(
        (ssm_term + other_terms).astype(jnp.bfloat16), (("grp", "seq_0", "seq_1"), "seq_2"), 1
    )
    hidden_out = (hidden_f + summed).astype(jnp.bfloat16)
    return (hidden_out, state_out)


def solution(mesh):
    torus = Mesh(
        mesh.devices.reshape(mesh.shape["grp"], 4, 4, 2), ("grp", "seq_0", "seq_1", "seq_2")
    )
    placed = (
        P(None, GRP_SEQ),
        P(),
        P(None, GRP_SEQ),
        P(None, GRP_SEQ),
        P(None, GRP_SEQ),
        P(GRP_SEQ),
        P(None, None, GRP_SEQ),
        P(GRP_SEQ, None),
        P(None, GRP_SEQ),
        P(GRP_SEQ),
        P(None, GRP_SEQ),
        P(GRP_SEQ),
        P(None, None, GRP_SEQ),
        P(GRP_SEQ, None),
        P(None, "grp"),
        P(None, "grp"),
        P(None, "grp"),
        P("grp", SEQ),
        P(None, GRP_SEQ),
        P(None, GRP_SEQ),
        P(GRP_SEQ, None),
        P(SEQ, None, None),
        P(),
    )
    return jax.shard_map(
        per_device,
        mesh=torus,
        in_specs=placed,
        out_specs=(P(None, GRP_SEQ), P(None, None, GRP_SEQ)),
        check_vma=False,
    )
```

profile of v0, /device:TPU:0, one launch (start us, length us, event | category | flops | bytes accessed | tf_op | source)
XLA Modules:
  0.0 155.4 jit_solution(11170985331494456441)
XLA Ops:
  0.6 1.7 %broadcast_in_dim.26 = bf16[64,96,32]{1,2,0:T(8,128)(2,1)} broadcast(bf16[96,32]{0,1:T(8,128)(2,1)} %param.23), dimensions={1,2} | broadcast | bytes 399360 | tf_op jit(solution)/shard_map/broadcast_in_dim | solution.py:19
  2.4 11.5 %all-to-all-start = ((bf16[64,96,32]{1,2,0:T(8,128)(2,1)}), bf16[64,96,32]{1,2,0:T(8,128)(2,1)S(1)}, u32[]{:S(2)}, u32[]{:S(2)}) async-start(bf16[64,96,32]{1,2,0:T(8,128)(2,1)} %broadcast_in_dim.26), calls=%async_computation | async-start | bytes 1048576 | tf_op jit(solution)/shard_map/all_to_all | solution.py:18
  13.9 0.7 fusion.43
  14.7 0.6 iota_compare_fusion
  15.3 0.7 multiply_cosine_fusion.1
  16.0 0.5 multiply_cosine_fusion
  16.6 4.1 %copy.50 = bf16[256,4096]{1,0:T(8,128)(2,1)} copy(bf16[256,4096]{0,1:T(8,128)(2,1)} %bitcast.65) | data formatting | bytes 4194304 | tf_op jit(solution)/shard_map/dot_general | solution.py:198
  20.7 9.8 %fusion = f32[3,512,2,128]{1,3,2,0:T(8,128)} fusion(bf16[2,128,4096,1]{2,1,0,3:T(8,128)(2,1)} %bitcast.67, bf16[3,512,4096]{2,1,0:T(8,128)(2,1)} %param.44), kind=kOutput, calls=%fused_computation | convolution fusion | flops 3221225472 | bytes 16252928 | tf_op jit(solution)/shard_map/dot_general | solution.py:198
  30.5 7.4 %convolution_convert_fusion = bf16[1536,256]{1,0:T(8,128)(2,1)} fusion(bf16[1536,4096]{1,0:T(8,128)(2,1)} %bitcast.78, bf16[4096,256]{1,0:T(8,128)(2,1)S(1)} %copy-done), kind=kOutput, calls=%fused_computation.6 | convolution fusion | flops 3221618688 | bytes 15466496 | tf_op jit(solution)/shard_map/dot_general | solution.py:203
  37.9 2.7 %reshape.189 = bf16[3,512,2,128]{3,2,1,0:T(2,128)(2,1)} reshape(bf16[1536,256]{1,0:T(8,128)(2,1)} %convolution_convert_fusion) | data formatting | bytes 1572864 | tf_op jit(solution)/shard_map/reshape | solution.py:205
  41.1 0.6 exp.29
  41.7 0.7 multiply_reduce_fusion.1
  42.4 2.6 %subtract_convert_fusion = (bf16[3,512,2,64]{1,3,2,0:T(8,128)(2,1)}, bf16[3,512,2,64]{1,3,2,0:T(8,128)(2,1)}) fusion(f32[3,512,2,128]{1,3,2,0:T(8,128)} %fusion, f32[3,512,64]{1,2,0:T(8,128)S(1)} %get-tuple-element.17, f32[3,512,64]{1,2,0:T(8,128)S(1)} %get-tuple-element.16), kind=kLoop, calls=%fused_computation.36 | loop fusion | flops 1572864 | bytes 3145728 | tf_op jit(solution)/shard_map/convert.9
  45.2 4.6 %all_to_all.50 = bf16[2,64,96,32]{2,3,1,0:T(8,128)(2,1)S(1)} all-to-all(bf16[2,64,96,32]{2,3,1,0:T(8,128)(2,1)S(1)} %broadcast_in_dim.27), channel_id=1, replica_groups=mesh['grp'=4,'seq_0'=4,'seq_1'=4,'seq_2'=2] {'seq_2'}, dimensions={0} | all-to-all | bytes 1572864 | tf_op jit(solution)/shard_map/all_to_all | solution.py:18
  50.3 0.6 fusion.3
  50.9 0.9 fusion.5
  51.9 1.0 fusion.14
  52.9 1.6 %fusion.12 = f32[3,256]{1,0:T(4,128)} fusion(bf16[4096,256]{1,0:T(8,128)(2,1)S(1)} %copy-done, bf16[96,4096]{0,1:T(8,128)(2,1)S(1)} %fusion.5, s32[]{:T(128)S(6)} %select_n.20), kind=kOutput, calls=%fused_computation.24 | convolution fusion | flops 6292992 | bytes 2886660 | tf_op jit(solution)/shard_map/dot_general | solution.py:191
  54.5 0.6 reshape.187
  55.1 3.3 %fusion.16 = f32[3,512]{1,0:T(4,128)S(1)} fusion(bf16[4096,512]{1,0:T(8,128)(2,1)} %param.37, bf16[96,4096]{0,1:T(8,128)(2,1)S(1)} %fusion.5, s32[]{:T(128)S(6)} %select_n.20), kind=kOutput, calls=%fused_computation.29 | convolution fusion | flops 12582912 | bytes 4986884 | tf_op jit(solution)/shard_map/dot_general | solution.py:179
  58.4 0.8 subtract_convert_fusion.2
  59.2 0.8 subtract_convert_fusion.1
  60.3 1.4 fusion.45
  61.7 0.6 copy-done.10
  62.3 0.8 fusion.32
  63.1 0.7 reshape.194
  63.8 1.7 %fusion.49 = f32[96,112]{1,0:T(8,128)S(1)} fusion(bf16[96,4096]{0,1:T(8,128)(2,1)S(1)} %fusion.5, bf16[4096,112]{0,1:T(8,128)(2,1)} %param.41), kind=kOutput, calls=%fused_computation.91 | convolution fusion | flops 88080384 | bytes 1746944 | tf_op jit(solution)/shard_map/dot_general | solution.py:164
  66.5 3.8 %all_to_all.51 = f32[2,64,216]{2,1,0:T(8,128)S(1)} all-to-all(f32[2,64,216]{2,1,0:T(8,128)S(1)} %bitcast.68), channel_id=1, replica_groups=mesh['grp'=4,'seq_0'=4,'seq_1'=4,'seq_2'=2] {'seq_2'}, dimensions={0} | all-to-all | bytes 221184 | tf_op jit(solution)/shard_map/all_to_all | solution.py:42
  70.4 0.7 all_to_all.34
  71.0 10.3 %all-to-all-start.3 = ((f32[64,1,216]{2,1,0:T(1,128)}), f32[64,1,216]{2,1,0:T(1,128)S(1)}, u32[]{:S(2)}, u32[]{:S(2)}) async-start(f32[64,1,216]{2,1,0:T(1,128)} %all_to_all.34), calls=%async_computation.3 | async-start | bytes 131072 | tf_op jit(solution)/shard_map/all_to_all | solution.py:49
  81.4 1.4 fusion.11
  82.8 8.1 %all-to-all-done.3 = f32[64,1,216]{2,1,0:T(1,128)S(1)} async-done(((f32[64,1,216]{2,1,0:T(1,128)}), f32[64,1,216]{2,1,0:T(1,128)S(1)}, u32[]{:S(2)}, u32[]{:S(2)}) %all-to-all-start.3) | async-done | bytes 55328 | tf_op jit(solution)/shard_map/all_to_all | solution.py:49
  91.0 0.7 broadcast_in_dim.34
  91.7 3.9 %all-to-all-start.6 = ((bf16[32,3,512]{2,1,0:T(4,128)(2,1)}), bf16[32,3,512]{2,1,0:T(4,128)(2,1)S(1)}, u32[]{:S(2)}, u32[]{:S(2)}) async-start(bf16[32,3,512]{2,1,0:T(4,128)(2,1)} %broadcast_in_dim.34), calls=%async_computation.6 | async-start | bytes 262144 | tf_op jit(solution)/shard_map/all_to_all | solution.py:18
  95.5 3.7 %fusion.9 = f32[96,4096]{1,0:T(8,128)} fusion(bf16[112,4096]{1,0:T(8,128)(2,1)} %param.43, bf16[96,4096]{0,1:T(8,128)(2,1)S(1)} %fusion.5, bf16[4096,112]{0,1:T(8,128)(2,1)} %param.42, f32[96,112]{1,0:T(8,128)S(1)} %fusion.49), kind=kOutput, calls=%fused_computation.19 | convolution fusion | flops 176225280 | bytes 4237312 | tf_op jit(solution)/shard_map/dot_general | solution.py:167
  99.4 4.0 %all-to-all-done.6 = bf16[32,3,512]{2,1,0:T(4,128)(2,1)S(1)} async-done(((bf16[32,3,512]{2,1,0:T(4,128)(2,1)}), bf16[32,3,512]{2,1,0:T(4,128)(2,1)S(1)}, u32[]{:S(2)}, u32[]{:S(2)}) %all-to-all-start.6) | async-done | bytes 98336 | tf_op jit(solution)/shard_map/all_to_all | solution.py:18
  103.4 0.7 broadcast_in_dim.28
  104.0 5.0 %all-to-all-start.4 = ((f32[64,1,216]{2,1,0:T(1,128)}), f32[64,1,216]{2,1,0:T(1,128)S(1)}, u32[]{:S(2)}, u32[]{:S(2)}) async-start(f32[64,1,216]{2,1,0:T(1,128)} %broadcast_in_dim.28), calls=%async_computation.4 | async-start | bytes 131072 | tf_op jit(solution)/shard_map/all_to_all | solution.py:18
  109.1 1.7 %fusion.6 = f32[96,4096]{1,0:T(8,128)} fusion(f32[96,4096]{1,0:T(8,128)} %fusion.9, s32[]{:T(128)S(6)} %select_n.19, bf16[96,512]{1,0:T(8,128)(2,1)S(1)} %reshape.190, bf16[512,128]{1,0:T(8,128)(2,1)} %param.40), kind=kOutput, calls=%fused_computation.12 | convolution fusion | flops 12595200 | bytes 327684 | tf_op jit(solution)/shard_map/dot_general | solution.py:231
  110.8 7.8 %all-to-all-done.4 = f32[64,1,216]{2,1,0:T(1,128)S(1)} async-done(((f32[64,1,216]{2,1,0:T(1,128)}), f32[64,1,216]{2,1,0:T(1,128)S(1)}, u32[]{:S(2)}, u32[]{:S(2)}) %all-to-all-start.4) | async-done | bytes 55328 | tf_op jit(solution)/shard_map/all_to_all | solution.py:18
  118.6 3.8 %all_to_all.52 = f32[2,64,216]{2,1,0:T(8,128)S(1)} all-to-all(f32[2,64,216]{2,1,0:T(8,128)S(1)} %broadcast_in_dim.30), channel_id=1, replica_groups=mesh['grp'=4,'seq_0'=4,'seq_1'=4,'seq_2'=2] {'seq_2'}, dimensions={0} | all-to-all | bytes 221184 | tf_op jit(solution)/shard_map/all_to_all | solution.py:18
  123.2 2.1 %multiply_reduce_fusion = (f32[96,64]{0,1:T(8,128)S(1)}, f32[96,16,64]{0,2,1:T(8,128)}) fusion(f32[96,16]{0,1:T(8,128)S(1)} %copy.39, f32[96,64]{0,1:T(8,128)S(1)} %divide_multiply_fusion, f32[96,16]{0,1:T(8,128)S(1)} %copy.38, f32[96,64]{0,1:T(8,128)S(1)} %get-tuple-element.23, f32[96,16,64]{0,2,1:T(8,128)} %param.35, f32[16,64]{1,0:T(8,128)S(1)} %copy-done.7, ...), kind=kLoop, calls=%fused_computation.39 | loop fusion | flops 681984 | bytes 901120 | tf_op jit(solution)/shard_map/reduce_sum | solution.py:161
  125.2 3.3 %fusion.2 = bf16[96,4096]{1,0:T(8,128)(2,1)} fusion(f32[96,4096]{1,0:T(8,128)} %fusion.6, bf16[64,4096]{1,0:T(8,128)(2,1)} %param.36, f32[96,64]{0,1:T(8,128)S(1)} %get-tuple-element.2, f32[96,64]{0,1:T(8,128)S(1)} %divide_multiply_fusion, f32[64]{0:T(128)S(1)} %copy-done.17, bf16[4096,64]{0,1:T(8,128)(2,1)} %param.26, bf16[96,4096]{0,1:T(8,128)(2,1)S(1)} %fusion.5), kind=kOutput, calls=%fused_computation.3 | convolution fusion | flops 101498880 | bytes 4243712 | tf_op jit(solution)/shard_map/dot_general | solution.py:163
  128.6 1.6 %copy.43 = bf16[96,4096]{0,1:T(8,128)(2,1)S(1)} copy(bf16[96,4096]{1,0:T(8,128)(2,1)} %fusion.2) | data formatting | bytes 1572864 | tf_op jit(solution)/shard_map/convert_element_type | solution.py:238
  130.2 4.6 %all_to_all.53 = bf16[2,64,96,32]{2,3,1,0:T(8,128)(2,1)S(1)} all-to-all(bf16[2,64,96,32]{2,3,1,0:T(8,128)(2,1)S(1)} %copy.44), channel_id=1, replica_groups=mesh['grp'=4,'seq_0'=4,'seq_1'=4,'seq_2'=2] {'seq_2'}, dimensions={0} | all-to-all | bytes 1572864 | tf_op jit(solution)/shard_map/all_to_all | solution.py:72
  134.8 1.3 reduce_sum.81
  136.1 18.5 %all_to_all.54 = bf16[64,96,32]{1,2,0:T(8,128)(2,1)S(1)} all-to-all(bf16[64,96,32]{1,2,0:T(8,128)(2,1)} %reduce_sum.81), channel_id=1, replica_groups=mesh['grp'=4,'seq_0'=4,'seq_1'=4,'seq_2'=2] {'grp','seq_0','seq_1'}, dimensions={0} | all-to-all | bytes 786432 | tf_op jit(solution)/shard_map/all_to_all | solution.py:80
  154.8 0.6 add_convert_fusion.1
  (71 shorter events, 3.8 us)
Async XLA Ops:
  0.6 29.8 %copy-start = (bf16[4096,256]{1,0:T(8,128)(2,1)S(1)}, bf16[4096,256]{1,0:T(8,128)(2,1)}, u32[]{:S(2)}) copy-start(bf16[4096,256]{1,0:T(8,128)(2,1)} %param.39) | copy-start | bytes 6291460
  2.4 42.7 %all-to-all-start = ((bf16[64,96,32]{1,2,0:T(8,128)(2,1)}), bf16[64,96,32]{1,2,0:T(8,128)(2,1)S(1)}, u32[]{:S(2)}, u32[]{:S(2)}) async-start(bf16[64,96,32]{1,2,0:T(8,128)(2,1)} %broadcast_in_dim.26), calls=%async_computation | async-start | bytes 1048576 | tf_op jit(solution)/shard_map/all_to_all | solution.py:18
  30.4 10.1 %copy-start.15 = (f32[4,64]{1,0:T(4,128)S(1)}, f32[4,64]{1,0:T(4,128)}, u32[]{:S(2)}) copy-start(f32[4,64]{1,0:T(4,128)} %param.27) | copy-start | bytes 3076
  30.4 10.7 %copy-start.14 = (f32[16,64]{1,0:T(8,128)S(1)}, f32[16,64]{1,0:T(8,128)}, u32[]{:S(2)}) copy-start(f32[16,64]{1,0:T(8,128)} %param.33) | copy-start | bytes 12292
  30.4 11.3 %copy-start.6 = (bf16[96,3,64]{0,2,1:T(8,128)(2,1)S(1)}, bf16[96,3,64]{0,2,1:T(8,128)(2,1)}, u32[]{:S(2)}) copy-start(bf16[96,3,64]{0,2,1:T(8,128)(2,1)} %param.29) | copy-start | bytes 110596
  50.0 0.8 copy-start.12
  50.3 1.6 %copy-start.1 = (bf16[4096,256]{1,0:T(8,128)(2,1)S(1)}, bf16[4096,256]{1,0:T(8,128)(2,1)}, u32[]{:S(2)}) copy-start(bf16[4096,256]{1,0:T(8,128)(2,1)} %param.38) | copy-start | bytes 6291460
  55.1 5.2 %copy-start.3 = (bf16[3,512,2,64]{1,3,2,0:T(8,128)(2,1)S(1)}, bf16[3,512,2,64]{1,3,2,0:T(8,128)(2,1)}, u32[]{:S(2)}) copy-start(bf16[3,512,2,64]{1,3,2,0:T(8,128)(2,1)} %get-tuple-element.8) | copy-start | bytes 1179652
  61.6 0.6 copy-start.10
  61.6 4.2 %copy-start.4 = (f32[96,64]{0,1:T(8,128)S(1)}, f32[96,64]{0,1:T(8,128)}, u32[]{:S(2)}) copy-start(f32[96,64]{0,1:T(8,128)} %multiply_reduce_fusion.1) | copy-start | bytes 73732
  61.6 4.2 %copy-start.18 = (f32[64]{0:T(128)S(1)}, f32[64]{0:T(128)}, u32[]{:S(2)}) copy-start(f32[64]{0:T(128)} %param.28) | copy-start | bytes 772
  61.7 4.2 %copy-start.19 = (f32[64]{0:T(128)S(1)}, f32[64]{0:T(128)}, u32[]{:S(2)}) copy-start(f32[64]{0:T(128)} %slice_bitcast_fusion) | copy-start | bytes 772
  61.7 4.3 %copy-start.5 = (bf16[64,288]{1,0:T(8,128)(2,1)S(1)}, bf16[64,288]{1,0:T(8,128)(2,1)}, u32[]{:S(2)}) copy-start(bf16[64,288]{1,0:T(8,128)(2,1)} %param.30) | copy-start | bytes 110596
  63.8 1.7 %copy-start.2 = (bf16[4096,64]{0,1:T(8,128)(2,1)S(1)}, bf16[4096,64]{0,1:T(8,128)(2,1)}, u32[]{:S(2)}) copy-start(bf16[4096,64]{0,1:T(8,128)(2,1)} %param.25) | copy-start | bytes 1572868
  63.8 17.6 %copy-start.11 = (f32[3,2,2,512]{3,2,1,0:T(2,128)S(1)}, f32[3,2,2,512]{3,2,1,0:T(2,128)}, u32[]{:S(2)}) copy-start(f32[3,2,2,512]{3,2,1,0:T(2,128)} %copy-done.10) | copy-start | bytes 73732
  63.8 17.6 %copy-start.13 = (pred[3,512]{1,0:T(4,128)(4,1)S(1)}, pred[3,512]{1,0:T(4,128)(4,1)}, u32[]{:S(2)}) copy-start(pred[3,512]{1,0:T(4,128)(4,1)} %iota_compare_fusion) | copy-start | bytes 4612
  71.0 19.9 %all-to-all-start.3 = ((f32[64,1,216]{2,1,0:T(1,128)}), f32[64,1,216]{2,1,0:T(1,128)S(1)}, u32[]{:S(2)}, u32[]{:S(2)}) async-start(f32[64,1,216]{2,1,0:T(1,128)} %all_to_all.34), calls=%async_computation.3 | async-start | bytes 131072 | tf_op jit(solution)/shard_map/all_to_all | solution.py:49
  91.7 11.7 %all-to-all-start.6 = ((bf16[32,3,512]{2,1,0:T(4,128)(2,1)}), bf16[32,3,512]{2,1,0:T(4,128)(2,1)S(1)}, u32[]{:S(2)}, u32[]{:S(2)}) async-start(bf16[32,3,512]{2,1,0:T(4,128)(2,1)} %broadcast_in_dim.34), calls=%async_computation.6 | async-start | bytes 262144 | tf_op jit(solution)/shard_map/all_to_all | solution.py:18
  99.3 23.7 %copy-start.9 = (bf16[256,64]{0,1:T(8,128)(2,1)S(1)}, bf16[256,64]{0,1:T(8,128)(2,1)}, u32[]{:S(2)}) copy-start(bf16[256,64]{0,1:T(8,128)(2,1)} %param.31) | copy-start | bytes 98308
  99.3 23.7 %copy-start.16 = (f32[64]{0:T(128)S(1)}, f32[64]{0:T(128)}, u32[]{:S(2)}) copy-start(f32[64]{0:T(128)} %param.32) | copy-start | bytes 772
  99.3 23.9 %copy-start.7 = (f32[16,64]{1,0:T(8,128)S(1)}, f32[16,64]{1,0:T(8,128)}, u32[]{:S(2)}) copy-start(f32[16,64]{1,0:T(8,128)} %exp.29) | copy-start | bytes 12292
  99.3 26.0 %copy-start.17 = (f32[64]{0:T(128)S(1)}, f32[64]{0:T(128)}, u32[]{:S(2)}) copy-start(f32[64]{0:T(128)} %param.34) | copy-start | bytes 772
  104.0 14.6 %all-to-all-start.4 = ((f32[64,1,216]{2,1,0:T(1,128)}), f32[64,1,216]{2,1,0:T(1,128)S(1)}, u32[]{:S(2)}, u32[]{:S(2)}) async-start(f32[64,1,216]{2,1,0:T(1,128)} %broadcast_in_dim.28), calls=%async_computation.4 | async-start | bytes 131072 | tf_op jit(solution)/shard_map/all_to_all | solution.py:18
  134.8 20.0 %copy-start.8 = (bf16[96,32]{0,1:T(8,128)(2,1)S(1)}, bf16[96,32]{0,1:T(8,128)(2,1)}, u32[]{:S(2)}) copy-start(bf16[96,32]{0,1:T(8,128)(2,1)} %param.23) | copy-start | bytes 18436
where the time goes:
time: 156 us; the launch traced here: 155 us
  matrix products  37.2 us (24%)
  blocking collectives  35.4 us (23%)
  starting transfers between devices  30.7 us (20%)
  waiting for transfers between devices  19.9 us (13%)
  local copies, waits for them, and re-layouts  16.8 us (11%)
  other arithmetic  14.5 us (9%)
    all_to_all x3, starting transfers between devices, from_everyone(): lax.all_to_all(jnp.broadcast_to(shard[None], (length, *shard.shape)), axi...  20.3 us
    all_to_all x1, blocking collectives, sum_in_two_steps(): lax.all_to_all(nearer.astype(jnp.bfloat16), far, split_axis=0, concat_axi...  18.5 us
    all_to_all x3, waiting for transfers between devices, from_everyone(): lax.all_to_all(jnp.broadcast_to(shard[None], (length, *shard.shape)), axi...  11.8 us
    all_to_all x1, starting transfers between devices, sum_by_axis(): return jnp.sum(lax.all_to_all(own, far, 0, 0, tiled=True), axis=0)  10.3 us
    dot_general x1, matrix products, per_device(): jnp.dot(flat_inputs, key_projection, preferred_element_type=jnp.float32)  9.77 us
    all_to_all x2, blocking collectives, from_everyone(): lax.all_to_all(jnp.broadcast_to(shard[None], (length, *shard.shape)), axi...  8.41 us
    all_to_all x1, waiting for transfers between devices, sum_by_axis(): return jnp.sum(lax.all_to_all(own, far, 0, 0, tiled=True), axis=0)  8.13 us
    dot_general x1, matrix products, per_device(): jnp.dot(flat_inputs, value_projection, preferred_element_type=jnp.float32)  7.42 us
  transfers between devices with their start and end apart: 4, of which 3 were waited for; matrix products, arithmetic and copies ran while one was open for 25% of the time, Pallas kernels for 0%

commit v1 on v0

v1 whole, which is shorter than its diff:
```python
import functools

import jax
import jax.numpy as jnp
import numpy as np
from jax import lax
from jax.experimental import pallas as pl
from jax.experimental.pallas import tpu as pltpu
from jax.sharding import Mesh
from jax.sharding import PartitionSpec as P

HEAD = 128
EPS = 1e-05
ROPE_BASE = 10000.0
MESH_ID = pl.DeviceIdType.MESH
F32, BF16 = jnp.float32, jnp.bfloat16
GRP_SEQ = ("grp", "seq_0", "seq_1", "seq_2")
SEQ = ("seq_0", "seq_1", "seq_2")
DOT_00 = (((0,), (0,)), ((), ()))
DOT_11 = (((1,), (1,)), ((), ()))
NAMES = (
    "hid", "gain", "w_in", "w_gate", "conv_w", "conv_b", "conv_st", "w_sp", "w_step", "step_b",
    "log_decay", "skip", "state", "w_so", "w_q", "w_k", "w_v", "w_ao", "w_mg", "w_mu", "w_md",
    "cached", "lens", "cos", "sin", "pick",
)


def silu(v):
    return v * jax.nn.sigmoid(v)


def rot(v, cosine, sine):
    return v * cosine + pltpu.roll(v, HEAD // 2, 1) * sine


def dot(a, b):
    return jnp.dot(a, b, preferred_element_type=F32)


def dot_g(a, b, dims):
    return lax.dot_general(a, b, dims, preferred_element_type=F32)


def kernel(sizes, *refs):
    nz, nx, ny, batch, own_seqs, window = sizes
    n_in = len(NAMES)
    r = dict(zip(NAMES, refs[:n_in]))
    out_ref, state_out = refs[n_in : n_in + 2]
    (
        X, XN, G, xb, wkv, wq, wst, wsp, wstep, wso, wmd, wao, kbuf, vbuf, cos, sin, pick,
        gain, conv_w, conv_b, conv_st, step_b, log_decay, skip, state, att_f, AT, LD, LR, LS, RL,
        LF, Pf, PB, R0, A1, B0, B1, A20, A21, C0, C1, A30, A31, D0, D1, gated, mlph,
        lsem, ags, agr, agds, agdr, ars, arr, ards, ardr, ats, atr, rss, rsr, rsds, rsdr,
    ) = refs[n_in + 2 :]
    nzx = nz * nx
    z, x = lax.axis_index("grp"), lax.axis_index("seq_0")
    y, c = lax.axis_index("seq_1"), lax.axis_index("seq_2")
    pc = 1 - c
    zx = z * nx + x
    seq = (x * ny + y) * 2 + c
    at = {"grp": z, "seq_0": x, "seq_1": y}
    count = {"grp": nz, "seq_0": nx, "seq_1": ny}
    ch = wst.shape[0]
    e_dim = wso.shape[0]
    ff = wmd.shape[0]
    sends = []

    def send(src, dst, ss, rs, axis, d):
        to = pc if axis == "seq_2" else lax.rem(at[axis] + d, count[axis])
        copy = pltpu.make_async_remote_copy(
            src_ref=src, dst_ref=dst, send_sem=ss, recv_sem=rs,
            device_id={axis: to}, device_id_type=MESH_ID,
        )
        copy.start()
        sends.append(copy)
        return copy

    def source(axis, d):
        return lax.rem(at[axis] + count[axis] - d, count[axis])

    local = {}

    def fetch(key, src, dst):
        copy = pltpu.make_async_copy(src, dst, lsem.at[len(local)])
        copy.start()
        local[key] = copy

    def ready(*keys):
        for key in keys:
            local[key].wait()

    for h in range(2):
        fetch(("hid", h), r["hid"].at[pl.ds(16 * h, 16)], X.at[h, c, zx, y])
    kvw = r["w_k"].shape[1]
    fetch("wk", r["w_k"], wkv.at[:, pl.ds(0, kvw)])
    fetch("wv", r["w_v"], wkv.at[:, pl.ds(kvw, kvw)])
    chunk = min(256, window)
    n_chunks = own_seqs * window // chunk
    for i in range(n_chunks):
        rows = pl.ds(i * chunk, chunk)
        fetch(("xb", i), r["cached"].at[rows], xb.at[rows])
        if i == 0:
            fetch("cos", r["cos"], cos)
            fetch("sin", r["sin"], sin)
    fetch("gain", r["gain"], gain)
    fetch("w_in", r["w_in"], wst.at[pl.ds(0, e_dim)])
    fetch("w_gate", r["w_gate"], wst.at[pl.ds(e_dim, e_dim)])
    for key, dst in (
        ("conv_w", conv_w), ("conv_b", conv_b), ("conv_st", conv_st), ("w_sp", wsp),
        ("step_b", step_b), ("log_decay", log_decay), ("skip", skip), ("w_q", wq),
    ):
        fetch(key, r[key], dst)
    fetch("w_mg", r["w_mg"], wst.at[pl.ds(2 * e_dim, ff)])
    fetch("w_mu", r["w_mu"], wst.at[pl.ds(2 * e_dim + ff, ff)])
    for key, dst in (
        ("w_md", wmd), ("w_step", wstep), ("state", state), ("w_so", wso), ("w_ao", wao), ("pick", pick),
    ):
        fetch(key, r[key], dst)

    barrier = pltpu.get_barrier_semaphore()
    for axis in ("grp", "seq_0", "seq_1"):
        for d in range(1, count[axis]):
            to = lax.rem(at[axis] + d, count[axis])
            pl.semaphore_signal(barrier, inc=1, device_id={axis: to}, device_id_type=MESH_ID)
    pl.semaphore_signal(barrier, inc=1, device_id={"seq_2": pc}, device_id_type=MESH_ID)
    pl.semaphore_wait(barrier, nz + nx + ny - 2)

    orders = (("seq_1", "seq_0", "grp"), ("seq_0", "grp", "seq_1"))

    def gathered(h, phase, zz, xx, yy):
        if phase == 0:
            return X.at[h, c, zz * nx + xx, yy]
        if h == 0:
            return X.at[0, c, zz * nx + xx] if phase == 1 else X.at[0, c, pl.ds(zz * nx, nx)]
        return X.at[1, c, pl.ds(zz * nx, nx), yy] if phase == 1 else X.at[1, c, :, yy]

    def gather_start(h, phase):
        ref = gathered(h, phase, z, x, y)
        axis = orders[h][phase]
        return [
            send(ref, ref, ags.at[h, phase, d - 1], agr.at[h, phase, d - 1], axis, d)
            for d in range(1, count[axis])
        ]

    ready(("hid", 0), ("hid", 1))
    gather = [gather_start(h, 0) for h in range(2)]

    def project(i, carry):
        rows = pl.ds(pl.multiple_of(i * chunk, chunk), chunk)
        kv = dot(xb[rows, :], wkv[...])
        place = pl.ds(pl.multiple_of(lax.rem(i, window // chunk) * chunk, chunk), chunk)
        cs, sn = cos[place, :], sin[place, :]
        for k in range(kvw // HEAD):
            cols = slice(k * HEAD, (k + 1) * HEAD)
            kbuf[rows, cols] = rot(kv[:, cols], cs, sn).astype(BF16)
        vbuf[rows, :] = kv[:, kvw:].astype(BF16)
        return carry

    def project_chunks(lo, hi):
        for i in range(lo, hi):
            ready(("xb", i))
        lax.fori_loop(lo, hi, project, 0)

    stop = (n_chunks // 3, n_chunks * 5 // 6)
    ready("wk", "wv", "cos", "sin")
    project_chunks(0, stop[0])
    for h in range(2):
        for copy in gather[h]:
            copy.wait_recv()
    gather = [gather_start(h, 1) for h in range(2)]
    project_chunks(stop[0], stop[1])
    for h in range(2):
        for copy in gather[h]:
            copy.wait_recv()
    gather = [gather_start(h, 2) for h in range(2)]
    across = []

    def cross(h, place, k):
        zz, yy = (place, y) if h == 0 else (z, place)
        ref = gathered(h, 2, zz, x, yy)
        across.append(send(ref, ref, agds.at[h, k], agdr.at[h, k], "seq_2", 0))

    cross(0, z, 0)
    cross(1, y, 0)
    project_chunks(stop[1], n_chunks)

    ready("gain", "conv_w", "conv_b", "conv_st", "w_sp", "step_b", "log_decay", "skip")
    for k in range(G.shape[0] // 128):
        G[k * 128 : (k + 1) * 128, :] = jnp.broadcast_to(gain[k : k + 1, :], (batch, 128)).T
    conv_wt = conv_w[...].T
    bias_col = conv_b[...].T
    step_col = step_b[...].T
    skip_col = skip[...].T
    decay = jnp.exp(log_decay[...]).T
    past = conv_wt[:, 0:1] * conv_st[0].astype(F32)
    for k in range(1, conv_st.shape[0]):
        past = past + conv_wt[:, k : k + 1] * conv_st[k].astype(F32)

    for k in (1, 3, 2):
        for h in range(2):
            axis = orders[h][2]
            if k < count[axis]:
                gather[h][k - 1].wait_recv()
                cross(h, source(axis, k), k)
    for copy in across:
        copy.wait_recv()

    def squares(i, acc):
        for h in range(2):
            for cc in range(2):
                for yy in range(ny):
                    v = X[h, cc, i, yy].astype(F32)
                    acc = acc + v * v
        return acc

    total = lax.fori_loop(0, nzx, squares, jnp.zeros((16, batch), F32))
    width = nzx * ny * 64
    scale = lax.rsqrt(jnp.sum(total, axis=0, keepdims=True) / width + EPS)

    def normalize(i, carry):
        for yy in range(ny):
            for cc in range(2):
                for h in range(2):
                    at_row = pl.multiple_of(i * (ny * 64), ny * 64) + (yy * 64 + cc * 32 + h * 16)
                    rows = pl.ds(pl.multiple_of(at_row, 16), 16)
                    v = X[h, cc, i, yy].astype(F32)
                    XN[rows, :] = (v * scale * G[rows, :]).astype(BF16)
        return carry

    lax.fori_loop(0, nzx, normalize, 0)

    ready("w_in", "w_gate")
    both = dot(wst[: 2 * e_dim, :], XN[...])
    ssm_in = both[:e_dim, :].astype(BF16).astype(F32)
    gate_in = both[e_dim:, :]
    conv_out = silu(bias_col + past + conv_wt[:, -1:] * ssm_in)
    low = dot_g(wsp[...], conv_out.astype(BF16), DOT_00)
    third = low.shape[0] // 6
    for cc in range(2):
        for t in range(3):
            LD[cc, t] = low[(cc * 3 + t) * third : (cc * 3 + t + 1) * third, :]
    low_first = send(LD.at[pc], LR, ards.at[0], ardr.at[0], "seq_2", 0)

    row = lax.broadcasted_iota(jnp.int32, (8, batch), 0)
    col = lax.broadcasted_iota(jnp.int32, (8, batch), 1)
    chosen = ((col == row + seq * own_seqs) & (row < own_seqs)).astype(F32).astype(BF16)
    fresh = dot_g(chosen, XN[...], DOT_11).astype(BF16)
    ready("w_q")
    query = dot(fresh, wq[...])
    new_kv = dot(fresh, wkv[...])

    low_first.wait_recv()
    for t in range(3):
        LS[0, t] = LD[c, t] + LR[t]
    ring = ("seq_0", "seq_1", "grp")

    def sum_start(phase):
        return [
            [
                send(LS.at[phase, t], RL.at[phase, t, d - 1], ars.at[phase, t, d - 1],
                     arr.at[phase, t, d - 1], ring[(t + phase) % 3], d)
                for d in range(1, count[ring[(t + phase) % 3]])
            ]
            for t in range(3)
        ]

    def sum_end(phase, copies):
        for t in range(3):
            value = LS[phase, t]
            for d, copy in enumerate(copies[t]):
                copy.wait_recv()
                value = value + RL[phase, t, d]
            if phase < 2:
                LS[phase + 1, t] = value
            else:
                LF[c, t] = value

    low_copies = sum_start(0)

    heads = query.shape[1] // HEAD
    kvs = kvw // HEAD
    per = heads // kvs
    row8 = lax.broadcasted_iota(jnp.int32, (8, HEAD), 0)
    slots = lax.broadcasted_iota(jnp.int32, (8, window), 1)
    cs = jnp.zeros((8, HEAD), F32)
    sn = jnp.zeros((8, HEAD), F32)
    lengths = []
    for b in range(own_seqs):
        length = r["lens"][seq * own_seqs + b]
        lengths.append(length)
        cs = jnp.where(row8 == b, cos[pl.ds(length, 1), :], cs)
        sn = jnp.where(row8 == b, sin[pl.ds(length, 1), :], sn)
    q_rot = [rot(query[:, h * HEAD : (h + 1) * HEAD], cs, sn).astype(BF16).astype(F32) for h in range(heads)]
    k_new = [rot(new_kv[:, k * HEAD : (k + 1) * HEAD], cs, sn).astype(BF16).astype(F32) for k in range(kvs)]
    v_new = [new_kv[:, kvw + k * HEAD : kvw + (k + 1) * HEAD].astype(BF16).astype(F32) for k in range(kvs)]
    unit = HEAD ** (-0.5)
    att_f[...] = jnp.zeros_like(att_f)
    for b in range(own_seqs):
        per_head = jnp.zeros((8, HEAD), F32)
        k_row = jnp.zeros((8, HEAD), F32)
        v_row = jnp.zeros((8, HEAD), F32)
        for h in range(heads):
            per_head = jnp.where(row8 == h, q_rot[h][b : b + 1, :], per_head)
            k_row = jnp.where(row8 == h, k_new[h // per][b : b + 1, :], k_row)
            v_row = jnp.where(row8 == h, v_new[h // per][b : b + 1, :], v_row)
        blocks = [jnp.where((row8 >= k * per) & (row8 < (k + 1) * per), per_head, 0.0) for k in range(kvs)]
        rows = slice(b * window, (b + 1) * window)
        scores = dot_g(jnp.concatenate(blocks, axis=1).astype(BF16), kbuf[rows, :], DOT_11) * unit
        fresh_score = jnp.sum(per_head * k_row, axis=1, keepdims=True) * unit
        valid = slots < lengths[b]
        scores = jnp.where(valid, scores, -1e30)
        top = jnp.maximum(jnp.max(scores, axis=1, keepdims=True), fresh_score)
        weights = jnp.where(valid, jnp.exp(scores - top), 0.0)
        weight_new = jnp.exp(fresh_score - top)
        all_weights = jnp.sum(weights, axis=1, keepdims=True) + weight_new
        mixed = dot(weights.astype(BF16), vbuf[rows, :])
        taken = mixed[:, :HEAD]
        for k in range(1, kvs):
            taken = jnp.where(row8 >= k * per, mixed[:, k * HEAD : (k + 1) * HEAD], taken)
        result = (taken + weight_new * v_row) / all_weights
        att_f[b * heads : (b + 1) * heads, :] = result[:heads, :]
    AT[c, x, y] = att_f[...].astype(BF16)

    def att_start(k):
        ref, axis = (AT.at[c, x, y], "seq_0") if k == 0 else (AT.at[c, :, y], "seq_1")
        return [send(ref, ref, ats.at[k, d - 1], atr.at[k, d - 1], axis, d) for d in range(1, count[axis])]

    att_copies = att_start(0)
    sum_end(0, low_copies)
    low_copies = sum_start(1)

    ready("w_mg", "w_mu")
    inner = dot(wst[2 * e_dim :, :], XN[...])
    mlph[...] = (silu(inner[:ff, :]) * inner[ff:, :]).astype(BF16)
    for copy in att_copies:
        copy.wait_recv()
    att_copies = att_start(1)
    sum_end(1, low_copies)
    low_copies = sum_start(2)
    ready("w_md")
    span = ny * 64

    def down(i, carry):
        rows = pl.ds(pl.multiple_of(i * span, span), span)
        Pf[rows, :] = dot_g(wmd[:, rows], mlph[...], DOT_00)
        return carry

    lax.fori_loop(0, nzx, down, 0)
    for copy in att_copies:
        copy.wait_recv()
    att_last = send(AT.at[c], AT.at[c], ats.at[2, 0], atr.at[2, 0], "seq_2", 0)
    sum_end(2, low_copies)
    low_last = send(LF.at[c], LF.at[c], ards.at[1], ardr.at[1], "seq_2", 0)

    ready("w_ao", "pick")
    att_last.wait_recv()
    everyone = AT[...].reshape(-1, HEAD)
    part = jnp.zeros((batch, wao.shape[1]), F32)
    for h in range(heads):
        of_head = dot(pick[h * batch : (h + 1) * batch, :], everyone).astype(BF16)
        part = part + dot(of_head, wao[h * HEAD : (h + 1) * HEAD, :])
    n_cols = wao.shape[1]
    rows = pl.ds(pl.multiple_of(seq * n_cols, n_cols), n_cols)
    Pf[rows, :] = Pf[rows, :] + part.T

    ready("w_step", "state", "w_so")
    low_last.wait_recv()
    low = LF[...].reshape(6 * third, batch)
    rank = wstep.shape[1]
    n_state = state.shape[0]
    raw_step = dot(wstep[...], low[:rank, :].astype(BF16)) + step_col
    step = jnp.maximum(raw_step, 0.0) + jnp.log1p(jnp.exp(-jnp.abs(raw_step)))
    driven = step * conv_out
    mix = skip_col * conv_out
    for n in range(n_state):
        new = jnp.exp(-step * decay[:, n : n + 1]) * state[n] + driven * low[rank + n : rank + n + 1, :]
        state[n] = new
        mix = mix + new * low[rank + n_state + n : rank + n_state + n + 1, :]
    gated[...] = (mix * silu(gate_in)).astype(BF16)
    put_state = pltpu.make_async_copy(state, state_out, lsem.at[len(local)])
    put_state.start()

    def branch(i, carry):
        rows = pl.ds(pl.multiple_of(i * span, span), span)
        value = (dot_g(wso[:, rows], gated[...], DOT_00) + Pf[rows, :]).astype(BF16)
        for yy in range(ny):
            for cc in range(2):
                for h in range(2):
                    lo = yy * 64 + cc * 32 + h * 16
                    PB[cc, h, i, yy] = value[lo : lo + 16, :]
        return carry

    places = [lax.rem(z + 1 + k, nz) for k in range(nz)]
    cross_sum = []
    for k, zz in enumerate(places):
        lax.fori_loop(zz * nx, zz * nx + nx, branch, 0)
        planes = pl.ds(zz * nx, nx)
        cross_sum.append(
            send(PB.at[pc, :, planes], R0.at[:, planes], rsds.at[k], rsdr.at[k], "seq_2", 0)
        )

    def joined(i, carry):
        for h in range(2):
            A1[h, i] = (PB[c, h, i].astype(F32) + R0[h, i].astype(F32)).astype(BF16)
        return carry

    def reduce_send(h, phase, d, src, dst):
        axis = orders[h][2 - phase]
        return send(src, dst, rss.at[h, phase, d - 1], rsr.at[h, phase, d - 1], axis, d)

    first = [[], []]
    for k, zz in enumerate(places):
        cross_sum[k].wait_recv()
        lax.fori_loop(zz * nx, zz * nx + nx, joined, 0)
        if k < nz - 1:
            first[0].append(reduce_send(0, 0, k + 1, A1.at[0, pl.ds(zz * nx, nx)], B0.at[k]))
    for d in range(1, ny):
        first[1].append(reduce_send(1, 0, d, A1.at[1, :, lax.rem(y + d, ny)], B1.at[d - 1]))

    for copy in first[0]:
        copy.wait_recv()
    for xx in range(nx):
        value = A1[0, z * nx + xx].astype(F32)
        for d in range(nz - 1):
            value = value + B0[d, xx].astype(F32)
        A20[xx] = value.astype(BF16)
    second = [[], []]
    for d in range(1, nx):
        second[0].append(reduce_send(0, 1, d, A20.at[lax.rem(x + d, nx)], C0.at[d - 1]))
    for copy in first[1]:
        copy.wait_recv()
    for zz in range(nz):
        value = A1[1, zz * nx : (zz + 1) * nx, y].astype(F32)
        for d in range(ny - 1):
            value = value + B1[d, zz * nx : (zz + 1) * nx].astype(F32)
        A21[zz] = value.astype(BF16)
    for d in range(1, nz):
        second[1].append(reduce_send(1, 1, d, A21.at[lax.rem(z + d, nz)], C1.at[d - 1]))

    last = [[], []]
    for copy in second[0]:
        copy.wait_recv()
    value = A20[x].astype(F32)
    for d in range(nx - 1):
        value = value + C0[d].astype(F32)
    A30[...] = value.astype(BF16)
    for d in range(1, ny):
        last[0].append(reduce_send(0, 2, d, A30.at[lax.rem(y + d, ny)], D0.at[d - 1]))
    for copy in second[1]:
        copy.wait_recv()
    value = A21[z].astype(F32)
    for d in range(nz - 1):
        value = value + C1[d].astype(F32)
    A31[...] = value.astype(BF16)
    for d in range(1, nx):
        last[1].append(reduce_send(1, 2, d, A31.at[lax.rem(x + d, nx)], D1.at[d - 1]))

    for h, kept, place, landed in ((0, A30, y, D0), (1, A31, x, D1)):
        for copy in last[h]:
            copy.wait_recv()
        value = kept[place].astype(F32)
        for d in range(len(last[h])):
            value = value + landed[d].astype(F32)
        out_ref[h * 16 : (h + 1) * 16, :] = value
    for copy in sends:
        copy.wait_send()
    put_state.wait()


def tables(window):
    freq = np.float64(ROPE_BASE) ** (-(np.arange(HEAD // 2, dtype=np.float64) * 2.0) / HEAD)
    rows = -(-(window + 1) // 8) * 8
    angles = np.arange(rows, dtype=np.float64)[:, None] * freq.astype(np.float32).astype(np.float64)
    cosine, sine = np.cos(angles), np.sin(angles)
    cosine = np.concatenate([cosine, cosine], axis=1).astype(np.float32)
    sine = np.concatenate([-sine, sine], axis=1).astype(np.float32)
    return cosine, sine


def picker(nx, ny, own_seqs, heads):
    n_seq = nx * ny * 2
    out = np.zeros((heads, n_seq, own_seqs, 2, nx, ny, 16), np.float32)
    for s in range(n_seq):
        xx, yy, cc = s // (2 * ny), (s // 2) % ny, s % 2
        for b in range(own_seqs):
            for h in range(heads):
                out[h, s, b, cc, xx, yy, b * heads + h] = 1.0
    return out.reshape(heads * n_seq * own_seqs, n_seq * 16)


def per_device(shape, *args):
    nz, nx, ny = shape
    (
        hidden_in, norm_gain, w_ssm_in, w_ssm_gate, conv_weight, conv_bias, conv_state,
        w_state_proj, w_step, step_bias, log_decay, skip_gain, ssm_state, w_ssm_out, w_query,
        key_projection, value_projection, w_attn_out, w_mlp_gate, w_mlp_up, w_mlp_down,
        cached_inputs, window_lengths,
    ) = args
    batch = hidden_in.shape[0]
    width = norm_gain.shape[0]
    own_seqs, window = cached_inputs.shape[:2]
    e_dim, ff = w_ssm_in.shape[1], w_mlp_gate.shape[1]
    heads = w_query.shape[1] // HEAD
    kvw = key_projection.shape[1]
    taps, n_state = conv_weight.shape[0], log_decay.shape[0]
    nzx, n_low = nz * nx, w_state_proj.shape[1]
    third = n_low // 6
    cosine, sine = tables(window)
    picked = picker(nx, ny, own_seqs, heads)
    operands = (
        hidden_in.T, norm_gain.reshape(-1, 128), w_ssm_in.T, w_ssm_gate.T, conv_weight,
        conv_bias.reshape(1, -1), conv_state.transpose(1, 2, 0), w_state_proj, w_step.T,
        step_bias.reshape(1, -1), log_decay, skip_gain.reshape(1, -1), ssm_state.transpose(1, 2, 0),
        w_ssm_out, w_query, key_projection, value_projection, w_attn_out, w_mlp_gate.T, w_mlp_up.T,
        w_mlp_down, cached_inputs.reshape(own_seqs * window, width), window_lengths,
        jnp.asarray(cosine), jnp.asarray(sine), jnp.asarray(picked, BF16),
    )
    in_specs = [
        pl.BlockSpec(memory_space=pltpu.SMEM if name == "lens" else pl.ANY) for name in NAMES
    ]
    V, DMA = pltpu.VMEM, pltpu.SemaphoreType.DMA
    tail = (16, batch)
    scratch = [
        V((2, 2, nzx, ny) + tail, BF16),
        V((width, batch), BF16),
        V((width, batch), F32),
        V((own_seqs * window, width), BF16),
        V((width, 2 * kvw), BF16),
        V(w_query.shape, BF16),
        V((2 * e_dim + 2 * ff, width), BF16),
        V(w_state_proj.shape, BF16),
        V(w_step.shape[::-1], BF16),
        V(w_ssm_out.shape, BF16),
        V(w_mlp_down.shape, BF16),
        V(w_attn_out.shape, BF16),
        V((own_seqs * window, kvw), BF16),
        V((own_seqs * window, kvw), BF16),
        V(cosine.shape, F32),
        V(sine.shape, F32),
        V(picked.shape, BF16),
        V((width // 128, 128), F32),
        V((taps, e_dim), F32),
        V((1, e_dim), F32),
        V((taps - 1, e_dim, batch), BF16),
        V((1, e_dim), F32),
        V((n_state, e_dim), F32),
        V((1, e_dim), F32),
        V((n_state, e_dim, batch), F32),
        V((16, HEAD), F32),
        V((2, nx, ny, 16, HEAD), BF16),
        V((2, 3, third, batch), F32),
        V((3, third, batch), F32),
        V((3, 3, third, batch), F32),
        V((3, 3, 3, third, batch), F32),
        V((2, 3, third, batch), F32),
        V((width, batch), F32),
        V((2, 2, nzx, ny) + tail, BF16),
        V((2, nzx, ny) + tail, BF16),
        V((2, nzx, ny) + tail, BF16),
        V((nz - 1, nx, ny) + tail, BF16),
        V((ny - 1, nzx) + tail, BF16),
        V((nx, ny) + tail, BF16),
        V((nz, nx) + tail, BF16),
        V((nx - 1, ny) + tail, BF16),
        V((nz - 1, nx) + tail, BF16),
        V((ny,) + tail, BF16),
        V((nx,) + tail, BF16),
        V((ny - 1,) + tail, BF16),
        V((nx - 1,) + tail, BF16),
        V((e_dim, batch), BF16),
        V((ff, batch), BF16),
        DMA((48,)),
        DMA((2, 3, 3)), DMA((2, 3, 3)), DMA((2, 4)), DMA((2, 4)),
        DMA((3, 3, 3)), DMA((3, 3, 3)), DMA((2,)), DMA((2,)),
        DMA((3, 3)), DMA((3, 3)),
        DMA((2, 3, 3)), DMA((2, 3, 3)), DMA((4,)), DMA((4,)),
    ]
    summed, state = pl.pallas_call(
        functools.partial(kernel, (nz, nx, ny, batch, own_seqs, window)),
        out_shape=(
            jax.ShapeDtypeStruct((width // (nzx * ny * 2), batch), F32),
            jax.ShapeDtypeStruct((n_state, e_dim, batch), F32),
        ),
        in_specs=in_specs,
        out_specs=(pl.BlockSpec(memory_space=pltpu.VMEM), pl.BlockSpec(memory_space=pl.ANY)),
        scratch_shapes=scratch,
        compiler_params=pltpu.CompilerParams(
            collective_id=0, has_side_effects=True, vmem_limit_bytes=62 * 1024 * 1024
        ),
        name="block",
    )(*operands)
    hidden_out = (hidden_in.T.astype(F32) + summed).astype(BF16)
    return hidden_out.T, state.transpose(2, 0, 1)


def solution(mesh):
    nx = ny = 4
    if mesh.shape["seq"] != nx * ny * 2:
        nx = ny = 2
    nz = mesh.shape["grp"]
    torus = Mesh(mesh.devices.reshape(nz, nx, ny, 2), GRP_SEQ)
    placed = (
        P(None, GRP_SEQ),
        P(),
        P(None, GRP_SEQ),
        P(None, GRP_SEQ),
        P(None, GRP_SEQ),
        P(GRP_SEQ),
        P(None, None, GRP_SEQ),
        P(GRP_SEQ, None),
        P(None, GRP_SEQ),
        P(GRP_SEQ),
        P(None, GRP_SEQ),
        P(GRP_SEQ),
        P(None, None, GRP_SEQ),
        P(GRP_SEQ, None),
        P(None, "grp"),
        P(None, "grp"),
        P(None, "grp"),
        P("grp", SEQ),
        P(None, GRP_SEQ),
        P(None, GRP_SEQ),
        P(GRP_SEQ, None),
        P(SEQ, None, None),
        P(),
    )
    return jax.shard_map(
        functools.partial(per_device, (nz, nx, ny)),
        mesh=torus,
        in_specs=placed,
        out_specs=(P(None, GRP_SEQ), P(None, None, GRP_SEQ)),
        check_vma=False,
    )
```

time: 156 us -> 62.4 us (0.40)
  Pallas kernels: 0 us -> 58.3 us
  matrix products: 37.2 us -> 0 us
  blocking collectives: 35.4 us -> 0 us
  starting transfers between devices: 30.7 us -> 0 us
  waiting for transfers between devices: 19.9 us -> 0 us
  local copies, waits for them, and re-layouts: 16.8 us -> 1.89 us
  other arithmetic: 14.5 us -> 1.32 us
    pallas_call x0 -> x1, Pallas kernels: none -> 58.3 us  [per_device(): pl.pallas_call(functools.partial(kernel, (nz, nx, ny, batch, own_seqs, wi...]
    dot_general x15 -> x0, matrix products: 37.2 us -> none  [the longest x1 9.77 us: per_device(): jnp.dot(flat_inputs, key_projection, preferred_element_type=jnp.float32)]
    all_to_all x5 -> x0, blocking collectives: 35.4 us -> none  [the longest x1 18.5 us: sum_in_two_steps(): lax.all_to_all(nearer.astype(jnp.bfloat16), far, split_axis=0, concat_axi...]
    all_to_all x4 -> x0, starting transfers between devices: 30.7 us -> none  [the longest x3 20.3 us: from_everyone(): lax.all_to_all(jnp.broadcast_to(shard[None], (length, *shard.shape)), axi...]
    all_to_all x4 -> x0, waiting for transfers between devices: 19.9 us -> none  [the longest x3 11.8 us: from_everyone(): lax.all_to_all(jnp.broadcast_to(shard[None], (length, *shard.shape)), axi...]
    reduce_sum x8 -> x0, other arithmetic: 5.68 us -> none  [the longest x1 2.07 us: per_device(): jnp.sum(state_out * output_map[:, :, None], axis=1) + skip_gain * conv_out]
    another operation x3 -> x0, other arithmetic: 4.21 us -> none
    dot_general x1 -> x0, local copies, waits for them, and re-layouts: 4.12 us -> none  [per_device(): jnp.dot(flat_inputs, key_projection, preferred_element_type=jnp.float32)]
  transfers between devices with their start and end apart: 4 -> 0, of which waited for: 3 -> 0; matrix products, arithmetic and copies ran while one was open for 25% -> 0% of each run, Pallas kernels for 0% -> 0%
where the time goes in v1:
time: 62.4 us; the launch traced here: 62.2 us
  Pallas kernels  58.3 us (93%)
  local copies, waits for them, and re-layouts  1.89 us (3%)
  other arithmetic  1.32 us (2%)
  between operations  0.66 us (1%)
    pallas_call x1, Pallas kernels, per_device(): pl.pallas_call(functools.partial(kernel, (nz, nx, ny, batch, own_seqs, wi...  58.3 us
    unnamed x3, local copies, waits for them, and re-layouts  1.89 us
    transpose x1, other arithmetic, per_device(): return (hidden_out.T, state.transpose(2, 0, 1))  1.32 us

profile of v1, /device:TPU:0, one launch (start us, length us, event | category | flops | bytes accessed | tf_op | source)
XLA Modules:
  0.0 62.2 jit_solution(13498965934702486798)
XLA Ops:
  0.6 0.0 copy-start
  0.7 58.3 %block.1 = (f32[32,96]{1,0:T(8,128)}, f32[16,64,96]{2,1,0:T(8,128)}) custom-call(bf16[32,96]{1,0:T(8,128)(2,1)} %bitcast.26, f32[32,128]{1,0:T(8,128)} %bitcast.27, bf16[64,4096]{1,0:T(8,128)(2,1)} %bitcast.20, bf16[64,4096]{1,0:T(8,128)(2,1)} %bitcast.21, f32[4,64]{1,0:T(4,128)} %refs_4_.1, f32[1,64]{1,0:T(1,128)} %bitcast.28, bf16[3,64,96]{2,1,0:T(8,128)(2,1)} %bitcast.24, ...), custom_call_target="tpu_custom_call" | custom-call | tf_op jit(solution)/shard_map/block/pallas_call | solution.py:578
  59.0 0.0 copy-done
  59.0 1.3 %fusion = bf16[96,32]{0,1:T(8,128)(2,1)} fusion(f32[32,96]{1,0:T(8,128)} %get-tuple-element.4, bf16[96,32]{0,1:T(8,128)(2,1)S(1)} %copy-done), kind=kLoop, calls=%fused_computation.1 | loop fusion | flops 9216 | bytes 24576 | tf_op jit(solution)/shard_map/transpose | solution.py:593
  60.3 1.9 %copy.29 = f32[96,16,64]{0,2,1:T(8,128)} copy(f32[96,16,64]{0,2,1:T(8,128)} %bitcast.23) | data formatting | bytes 786432
Async XLA Ops:
  0.6 58.3 %copy-start = (bf16[96,32]{0,1:T(8,128)(2,1)S(1)}, bf16[96,32]{0,1:T(8,128)(2,1)}, u32[]{:S(2)}) copy-start(bf16[96,32]{0,1:T(8,128)(2,1)} %param.26) | copy-start | bytes 18436
